TPU v7x, 256 devices: a whole 4x4x8 slice. The times are simulated.
256 devices in a mesh: leaf: 256 (over z, x, y, core).
Axes of the slice: x: 4, y: 4, z: 8, core: 2. Of those that a mesh axis runs over, the one named last changes fastest.
Arguments:
- right_sides: bfloat16 [32, 524288], P(None, 'leaf'), may hold values from -6 to 6
- point_order: int32 [256, 2048], P('leaf'), may hold values from 0 to 2047, each once within a row
- leaf_inverse: bfloat16 [524288, 2048], P('leaf'), may hold values from -0.09375 to 0.09375
- basis_in: bfloat16 [524288, 256], P('leaf'), may hold values from -0.125 to 0.125
- basis_out: bfloat16 [65536, 2048], P('leaf'), may hold values from -0.1875 to 0.1875
- leaf_up: bfloat16 [65536, 256], P('leaf'), may hold values from -0.25 to 0.25
- leaf_down: bfloat16 [65536, 256], P('leaf'), may hold values from -0.3125 to 0.3125
- node_up: bfloat16 [65536, 256], P('leaf'), may hold values from -0.25 to 0.25
- node_down: bfloat16 [65536, 256], P('leaf'), may hold values from -0.3125 to 0.3125
- node_cross: bfloat16 [131072, 256], P('leaf'), may hold values from -0.25 to 0.25
- leaf_map: int32 [256], replicated, may hold values from 0 to 255, as said below
Outputs:
- solution: float32 [32, 524288], P(None, 'leaf')
Inputs may be any that keep to these rules, and one draw needn't show every extreme that they name: `point_order`: each row is a permutation of the leaf's columns. `leaf_map`: A permutation of the tree positions that keeps every device's leaf inside the device's aligned block of 4 devices.
All inputs are finite; a program needn't handle non-finite values.
Results may differ from a plain program's by a relative error of at most 0.015.
Values may be sent and summed in bfloat16 or wider, within the bound.
A program may use at most 192 MiB of HBM per device.

v0:
```python
import jax
import jax.numpy as jnp
from jax import lax
from jax.sharding import PartitionSpec as P

SPREAD = 4


def swapped(block, axis, apart):
    count = lax.axis_size(axis)
    route = []
    for low in range(count):
        high = low | 1 << apart
        if high != low and high < count:
            route += [(low, high), (high, low)]
    return lax.ppermute(block, axis, route)


def block_rise(value, self_index, depth_bits):
    collected = value[None]
    for bit_index in range(depth_bits):
        partner = swapped(collected, "leaf", bit_index)
        upper_bit = self_index >> bit_index & 1
        collected = jnp.where(
            upper_bit == 1,
            jnp.concatenate([partner, collected], 0),
            jnp.concatenate([collected, partner], 0),
        )
    return collected


def block_fall(value, self_index, depth_bits):
    collected = value[None]
    for bit_index in range(depth_bits):
        partner = swapped(collected, "leaf", bit_index)
        upper_bit = self_index >> bit_index & 1
        collected = jnp.where(
            upper_bit == 1,
            jnp.concatenate([partner, collected], 0),
            jnp.concatenate([collected, partner], 0),
        )
    return collected


def spread_node_maps(own_block, self_index, height_count):
    entries = []
    for height in range(1, height_count + 1):
        owning = self_index & (1 << height) - 1 == 1 << height - 1
        entries.append(jnp.where(owning, own_block, jnp.zeros_like(own_block)))
    stacked = jnp.stack(entries)
    for bit_index in range(height_count):
        moving = stacked[bit_index:]
        partner = swapped(moving, "leaf", bit_index)
        heights = jnp.arange(bit_index + 1, height_count + 1, dtype=jnp.int32)
        anchor = jnp.left_shift(jnp.right_shift(self_index, heights), heights) + jnp.left_shift(
            jnp.int32(1), heights - 1
        )
        taking = jnp.right_shift(jnp.bitwise_xor(self_index, anchor), bit_index) == 1
        updated = jnp.where(taking[:, None, None], partner, moving)
        stacked = jnp.concatenate([stacked[:bit_index], updated], 0)
    return stacked


def body(
    right_sides,
    point_order,
    leaf_inverse,
    basis_in,
    basis_out,
    leaf_up,
    leaf_down,
    node_up,
    node_down,
    node_cross,
    leaf_map,
):
    members = lax.axis_size("leaf")
    levels = members.bit_length() - 1
    depth_bits = SPREAD.bit_length() - 1
    self_index = lax.axis_index("leaf")
    rank_rows = leaf_up.shape[0]
    ordering = point_order[0]
    tree_rhs = jnp.take(right_sides, ordering, axis=1)
    near = jnp.dot(tree_rhs, leaf_inverse, preferred_element_type=jnp.float32)
    reduced = jnp.dot(tree_rhs, basis_in, preferred_element_type=jnp.float32).astype(jnp.bfloat16)
    slot_ids = jnp.arange(members, dtype=jnp.int32)
    source = jnp.sum(jnp.where(leaf_map == self_index, slot_ids, 0))
    position = jnp.sum(jnp.where(slot_ids == self_index, leaf_map, 0))
    collected = block_rise(reduced, self_index, depth_bits)
    node_g = lax.dynamic_index_in_dim(collected, source % SPREAD, 0, keepdims=False)
    own_block = jnp.concatenate([node_up, node_down, node_cross], 0)
    ancestry = spread_node_maps(own_block, self_index, levels)
    stored = []
    for height in range(1, levels + 1):
        if height == 1:
            child_up = leaf_up
        else:
            child_up = ancestry[height - 2, :rank_rows]
        product = jnp.dot(node_g, child_up, preferred_element_type=jnp.float32)
        payload = jnp.stack([node_g.astype(jnp.float32), product])
        partner = swapped(payload, "leaf", height - 1)
        stored.append(partner[0].astype(jnp.bfloat16))
        node_g = (product + partner[1]).astype(jnp.bfloat16)
    node_f = jnp.dot(
        node_g, ancestry[levels - 1, :rank_rows], preferred_element_type=jnp.float32
    ).astype(jnp.bfloat16)
    for height in range(levels, 0, -1):
        other_g = stored[height - 1]
        side_bit = self_index >> height - 1 & 1
        cross_rows = ancestry[height - 1, 2 * rank_rows :]
        coupling = jnp.where(side_bit == 0, cross_rows[:rank_rows], cross_rows[rank_rows:])
        if height == 1:
            child_down = leaf_down
        else:
            child_down = ancestry[height - 2, rank_rows : 2 * rank_rows]
        node_f = (
            jnp.dot(other_g, coupling, preferred_element_type=jnp.float32)
            + jnp.dot(node_f, child_down, preferred_element_type=jnp.float32)
        ).astype(jnp.bfloat16)
    collected_f = block_fall(node_f, self_index, depth_bits)
    leaf_f = lax.dynamic_index_in_dim(collected_f, position % SPREAD, 0, keepdims=False)
    answer = near + jnp.dot(leaf_f, basis_out, preferred_element_type=jnp.float32)
    return jnp.zeros_like(answer).at[:, ordering].set(answer)


def solution(mesh):
    placed = (
        P(None, "leaf"),
        P("leaf", None),
        P("leaf", None),
        P("leaf", None),
        P("leaf", None),
        P("leaf", None),
        P("leaf", None),
        P("leaf", None),
        P("leaf", None),
        P("leaf", None),
        P(),
    )
    return jax.shard_map(
        body, mesh=mesh, in_specs=placed, out_specs=P(None, "leaf"), check_vma=False
    )
```

profile of v0, /device:TPU:11, one launch (start us, length us, event | category | flops | bytes accessed | tf_op | source)
XLA Modules:
  0.0 427.4 jit_solution(972241906790659030)
XLA Ops:
  0.0 2.0 select_dynamic-update-slice_fusion.7
  2.1 1.9 select_dynamic-update-slice_fusion.6
  4.0 1.9 select_dynamic-update-slice_fusion.5
  11.2 7.0 %collective-permute-done.3 = bf16[8,1024,256]{2,1,0:T(8,128)(2,1)S(1)} collective-permute-done((bf16[8,1024,256]{2,1,0:T(8,128)(2,1)}, bf16[8,1024,256]{2,1,0:T(8,128)(2,1)S(1)}, u32[]{:S(2)}, u32[]{:S(2)}) %collective-permute-start.3) | collective-permute-done | bytes 4194336 | tf_op jit(solution)/shard_map/ppermute | solution.py:16
  18.1 2.8 broadcast_select_fusion
  21.5 80.3 %collective-permute-done.5 = bf16[7,1024,256]{2,1,0:T(8,128)(2,1)S(1)} collective-permute-done((bf16[7,1024,256]{2,1,0:T(8,128)(2,1)S(1)}, bf16[7,1024,256]{2,1,0:T(8,128)(2,1)S(1)}, u32[]{:S(2)}, u32[]{:S(2)}) %collective-permute-start.5) | collective-permute-done | bytes 3670048 | tf_op jit(solution)/shard_map/ppermute | solution.py:16
  102.5 2.1 collective-permute-start.7
  104.6 67.9 %collective-permute-done.7 = bf16[6,1024,256]{2,1,0:T(8,128)(2,1)S(1)} collective-permute-done((bf16[6,1024,256]{2,1,0:T(8,128)(2,1)S(1)}, bf16[6,1024,256]{2,1,0:T(8,128)(2,1)S(1)}, u32[]{:S(2)}, u32[]{:S(2)}) %collective-permute-start.7) | collective-permute-done | bytes 3145760 | tf_op jit(solution)/shard_map/ppermute | solution.py:16
  173.1 1.3 collective-permute-start.9
  174.5 55.1 %collective-permute-done.9 = bf16[5,1024,256]{2,1,0:T(8,128)(2,1)S(1)} collective-permute-done((bf16[5,1024,256]{2,1,0:T(8,128)(2,1)S(1)}, bf16[5,1024,256]{2,1,0:T(8,128)(2,1)S(1)}, u32[]{:S(2)}, u32[]{:S(2)}) %collective-permute-start.9) | collective-permute-done | bytes 2621472 | tf_op jit(solution)/shard_map/ppermute | solution.py:16
  230.0 1.5 slice.503
  232.2 1.8 collective-permute-start.11
  234.3 6.2 %gather_fusion = bf16[2048,32]{1,0:T(8,128)(2,1)S(1)} fusion(bf16[32,2048]{0,1:T(8,128)(2,1)S(1)} %copy.15, s32[2048]{0:T(1024)S(1)} %broadcast_clamp_fusion), kind=kCustom, calls=%fused_computation | custom fusion | bytes 270336 | tf_op jit(solution)/shard_map/jit(_take)/gather | solution.py:83
  241.1 3.3 collective-permute-start
  248.6 1.2 collective-permute-start.2
  252.5 2.9 collective-permute-done.4
  255.4 22.8 %collective-permute-done.11 = bf16[4,1024,256]{2,1,0:T(8,128)(2,1)} collective-permute-done((bf16[4,1024,256]{2,1,0:T(8,128)(2,1)}, bf16[4,1024,256]{2,1,0:T(8,128)(2,1)}, u32[]{:S(2)}, u32[]{:S(2)}) %collective-permute-start.11) | collective-permute-done | bytes 2097184 | tf_op jit(solution)/shard_map/ppermute | solution.py:16
  278.2 2.5 broadcast_select_fusion.4
  280.7 1.2 slice.509
  282.0 1.6 collective-permute-start.13
  284.7 2.1 collective-permute-start.6
  286.8 2.6 collective-permute-done.6
  289.4 1.0 fusion.51
  290.7 3.2 collective-permute-done.8
  294.0 1.0 fusion.45
  295.1 2.1 collective-permute-start.10
  297.1 17.7 %collective-permute-done.13 = bf16[3,1024,256]{2,1,0:T(8,128)(2,1)} collective-permute-done((bf16[3,1024,256]{2,1,0:T(8,128)(2,1)}, bf16[3,1024,256]{2,1,0:T(8,128)(2,1)}, u32[]{:S(2)}, u32[]{:S(2)}) %collective-permute-start.13) | collective-permute-done | bytes 1572896 | tf_op jit(solution)/shard_map/ppermute | solution.py:16
  314.8 1.6 broadcast_select_fusion.5
  316.5 3.1 collective-permute-start.15
  319.8 1.3 collective-permute-start.12
  321.1 18.0 %collective-permute-done.12 = f32[2,32,256]{2,1,0:T(8,128)S(1)} collective-permute-done((f32[2,32,256]{2,1,0:T(8,128)S(1)}, f32[2,32,256]{2,1,0:T(8,128)S(1)}, u32[]{:S(2)}, u32[]{:S(2)}) %collective-permute-start.12) | collective-permute-done | bytes 65568 | tf_op jit(solution)/shard_map/ppermute | solution.py:16
  339.3 2.2 collective-permute-start.14
  341.5 24.6 %collective-permute-done.15 = bf16[2,1024,256]{2,1,0:T(8,128)(2,1)S(1)} collective-permute-done((bf16[2,1024,256]{2,1,0:T(8,128)(2,1)S(1)}, bf16[2,1024,256]{2,1,0:T(8,128)(2,1)S(1)}, u32[]{:S(2)}, u32[]{:S(2)}) %collective-permute-start.15) | collective-permute-done | bytes 1048608 | tf_op jit(solution)/shard_map/ppermute | solution.py:16
  366.4 6.6 %collective-permute-start.17 = (bf16[1,1024,256]{2,1,0:T(8,128)(2,1)S(1)}, bf16[1,1024,256]{2,1,0:T(8,128)(2,1)S(1)}, u32[]{:S(2)}, u32[]{:S(2)}) collective-permute-start(bf16[1,1024,256]{2,1,0:T(8,128)(2,1)S(1)} %slice.521), channel_id=1, source_target_pairs={{0,128},{128,0},{1,129},{129,1},{2,130},{130,2},{3,131},{131,3},{4... | collective-permute-start | bytes 1572872 | tf_op jit(solution)/shard_map/ppermute | solution.py:16
  373.1 1.1 collective-permute-start.16
  374.2 22.0 %collective-permute-done.17 = bf16[1,1024,256]{2,1,0:T(8,128)(2,1)S(1)} collective-permute-done((bf16[1,1024,256]{2,1,0:T(8,128)(2,1)S(1)}, bf16[1,1024,256]{2,1,0:T(8,128)(2,1)S(1)}, u32[]{:S(2)}, u32[]{:S(2)}) %collective-permute-start.17) | collective-permute-done | bytes 524320 | tf_op jit(solution)/shard_map/ppermute | solution.py:16
  397.6 1.3 fusion.10
  398.8 1.3 fusion.11
  400.1 1.3 fusion.12
  401.4 1.3 fusion.13
  402.7 1.2 fusion.14
  403.9 1.3 fusion.15
  405.2 1.3 fusion.16
  406.5 1.3 fusion.17
  407.8 1.1 fusion.18
  409.0 2.8 collective-permute-start.18
  412.7 5.2 %fusion.21 = f32[32,2048]{1,0:T(8,128)S(1)} fusion(bf16[2048,2048]{1,0:T(8,128)(2,1)} %param.13, bf16[2048,32]{1,0:T(8,128)(2,1)} %copy-done.10, pred[2048]{0:T(1024)(128)(4,1)S(1)} %compare_and_fusion), kind=kOutput, calls=%fused_computation.52 | convolution fusion | flops 268500992 | bytes 8783872 | tf_op jit(solution)/shard_map/dot_general | solution.py:84
  420.5 5.8 %scatter_custom_fusion = f32[32,2048]{0,1:T(8,128)S(1)} fusion(s32[2048]{0:T(1024)S(1)} %bitcast.261, f32[2048,32]{1,0:T(8,128)S(1)} %copy.16, f32[]{:T(128)} %constant.37.clone.1), kind=kCustom, calls=%fused_computation.48 | custom fusion | bytes 262148 | tf_op jit(solution)/shard_map/scatter | solution.py:123
  (107 shorter events, 20.0 us)
Async XLA Ops:
  0.0 419.9 %copy-start = (bf16[256,2048]{1,0:T(8,128)(2,1)S(1)}, bf16[256,2048]{1,0:T(8,128)(2,1)}, u32[]{:S(2)}) copy-start(bf16[256,2048]{1,0:T(8,128)(2,1)} %param.15) | copy-start | bytes 3145732
  0.0 6.0 %copy-start.5 = (bf16[512,256]{1,0:T(8,128)(2,1)S(1)}, bf16[512,256]{1,0:T(8,128)(2,1)}, u32[]{:S(2)}) copy-start(bf16[512,256]{1,0:T(8,128)(2,1)} %param.20) | copy-start | bytes 786436
  0.0 6.0 %copy-start.7 = (bf16[256,256]{1,0:T(8,128)(2,1)S(1)}, bf16[256,256]{1,0:T(8,128)(2,1)}, u32[]{:S(2)}) copy-start(bf16[256,256]{1,0:T(8,128)(2,1)} %param.19) | copy-start | bytes 393220
  0.0 6.0 %copy-start.8 = (bf16[256,256]{1,0:T(8,128)(2,1)S(1)}, bf16[256,256]{1,0:T(8,128)(2,1)}, u32[]{:S(2)}) copy-start(bf16[256,256]{1,0:T(8,128)(2,1)} %param.18) | copy-start | bytes 393220
  10.5 7.7 %collective-permute-start.3 = (bf16[8,1024,256]{2,1,0:T(8,128)(2,1)}, bf16[8,1024,256]{2,1,0:T(8,128)(2,1)S(1)}, u32[]{:S(2)}, u32[]{:S(2)}) collective-permute-start(bf16[8,1024,256]{2,1,0:T(8,128)(2,1)} %select_dynamic-update-slice_fusion), channel_id=1, source_target_pairs={{0,1},{1,0},{2,3},{3,2},{4,5},{5,4},{6,7},{7,6},{8,9},{9,8},{10,11... | collective-permute-start | bytes 12582920 | tf_op jit(solution)/shard_map/ppermute | solution.py:16
  20.9 80.9 %copy-start.1 = (bf16[8,1024,256]{2,1,0:T(8,128)(2,1)}, bf16[8,1024,256]{2,1,0:T(8,128)(2,1)S(1)}, u32[]{:S(2)}) copy-start(bf16[8,1024,256]{2,1,0:T(8,128)(2,1)S(1)} %broadcast_select_fusion) | copy-start | bytes 12582916
  21.2 80.6 %collective-permute-start.5 = (bf16[7,1024,256]{2,1,0:T(8,128)(2,1)S(1)}, bf16[7,1024,256]{2,1,0:T(8,128)(2,1)S(1)}, u32[]{:S(2)}, u32[]{:S(2)}) collective-permute-start(bf16[7,1024,256]{2,1,0:T(8,128)(2,1)S(1)} %slice.485), channel_id=1, source_target_pairs={{0,2},{2,0},{1,3},{3,1},{4,6},{6,4},{5,7},{7,5},{8,10},{10,8},{9,1... | collective-permute-start | bytes 11010056 | tf_op jit(solution)/shard_map/ppermute | solution.py:16
  102.3 70.2 %copy-start.2 = (bf16[7,1024,256]{2,1,0:T(8,128)(2,1)}, bf16[7,1024,256]{2,1,0:T(8,128)(2,1)S(1)}, u32[]{:S(2)}) copy-start(bf16[7,1024,256]{2,1,0:T(8,128)(2,1)S(1)} %broadcast_select_fusion.1) | copy-start | bytes 11010052
  102.5 70.0 %collective-permute-start.7 = (bf16[6,1024,256]{2,1,0:T(8,128)(2,1)S(1)}, bf16[6,1024,256]{2,1,0:T(8,128)(2,1)S(1)}, u32[]{:S(2)}, u32[]{:S(2)}) collective-permute-start(bf16[6,1024,256]{2,1,0:T(8,128)(2,1)S(1)} %slice.491), channel_id=1, source_target_pairs={{0,4},{4,0},{1,5},{5,1},{2,6},{6,2},{3,7},{7,3},{8,12},{12,8},{9,1... | collective-permute-start | bytes 9437192 | tf_op jit(solution)/shard_map/ppermute | solution.py:16
  172.9 57.0 %copy-start.3 = (bf16[6,1024,256]{2,1,0:T(8,128)(2,1)}, bf16[6,1024,256]{2,1,0:T(8,128)(2,1)S(1)}, u32[]{:S(2)}) copy-start(bf16[6,1024,256]{2,1,0:T(8,128)(2,1)S(1)} %broadcast_select_fusion.2) | copy-start | bytes 9437188
  172.9 1.5 copy-start.14
  173.1 56.4 %collective-permute-start.9 = (bf16[5,1024,256]{2,1,0:T(8,128)(2,1)S(1)}, bf16[5,1024,256]{2,1,0:T(8,128)(2,1)S(1)}, u32[]{:S(2)}, u32[]{:S(2)}) collective-permute-start(bf16[5,1024,256]{2,1,0:T(8,128)(2,1)S(1)} %slice.497), channel_id=1, source_target_pairs={{0,8},{8,0},{1,9},{9,1},{2,10},{10,2},{3,11},{11,3},{4,12},{12,4},... | collective-permute-start | bytes 7864328 | tf_op jit(solution)/shard_map/ppermute | solution.py:16
  229.9 2.3 copy-start.4
  229.9 4.1 copy-start.12
  229.9 10.6 %copy-start.11 = (bf16[2048,256]{1,0:T(8,128)(2,1)S(1)}, bf16[2048,256]{1,0:T(8,128)(2,1)}, u32[]{:S(2)}) copy-start(bf16[2048,256]{1,0:T(8,128)(2,1)} %param.14) | copy-start | bytes 3145732
  229.9 15.5 %copy-start.18 = (s32[256]{0:T(256)S(1)}, s32[256]{0:T(256)}, u32[]{:S(2)}) copy-start(s32[256]{0:T(256)} %param.21) | copy-start | bytes 3076
  229.9 18.5 %copy-start.13 = (bf16[256,256]{1,0:T(8,128)(2,1)S(1)}, bf16[256,256]{1,0:T(8,128)(2,1)}, u32[]{:S(2)}) copy-start(bf16[256,256]{1,0:T(8,128)(2,1)} %param.16) | copy-start | bytes 393220
  232.2 46.1 %collective-permute-start.11 = (bf16[4,1024,256]{2,1,0:T(8,128)(2,1)}, bf16[4,1024,256]{2,1,0:T(8,128)(2,1)}, u32[]{:S(2)}, u32[]{:S(2)}) collective-permute-start(bf16[4,1024,256]{2,1,0:T(8,128)(2,1)} %slice.503), channel_id=1, source_target_pairs={{0,16},{16,0},{1,17},{17,1},{2,18},{18,2},{3,19},{19,3},{4,20},{20... | collective-permute-start | bytes 6291464 | tf_op jit(solution)/shard_map/ppermute | solution.py:16
  240.5 14.9 %copy-start.10 = (bf16[2048,32]{1,0:T(8,128)(2,1)}, bf16[2048,32]{1,0:T(8,128)(2,1)S(1)}, u32[]{:S(2)}) copy-start(bf16[2048,32]{1,0:T(8,128)(2,1)S(1)} %gather_fusion) | copy-start | bytes 393220
  241.1 4.1 collective-permute-start
  245.3 3.2 collective-permute-start.1
  248.6 2.1 collective-permute-start.2
  251.8 3.6 collective-permute-start.4
  282.0 32.8 %collective-permute-start.13 = (bf16[3,1024,256]{2,1,0:T(8,128)(2,1)}, bf16[3,1024,256]{2,1,0:T(8,128)(2,1)}, u32[]{:S(2)}, u32[]{:S(2)}) collective-permute-start(bf16[3,1024,256]{2,1,0:T(8,128)(2,1)} %slice.509), channel_id=1, source_target_pairs={{0,32},{32,0},{1,33},{33,1},{2,34},{34,2},{3,35},{35,3},{4,36},{36... | collective-permute-start | bytes 4718600 | tf_op jit(solution)/shard_map/ppermute | solution.py:16
  284.7 4.7 %collective-permute-start.6 = (f32[2,32,256]{2,1,0:T(8,128)S(1)}, f32[2,32,256]{2,1,0:T(8,128)S(1)}, u32[]{:S(2)}, u32[]{:S(2)}) collective-permute-start(f32[2,32,256]{2,1,0:T(8,128)S(1)} %pad_maximum_fusion.3), channel_id=1, source_target_pairs={{0,4},{4,0},{1,5},{5,1},{2,6},{6,2},{3,7},{7,3},{8,12},{12,8},{9,1... | collective-permute-start | bytes 196616 | tf_op jit(solution)/shard_map/ppermute | solution.py:16
  290.4 3.6 collective-permute-start.8
  295.1 24.6 %collective-permute-start.10 = (f32[2,32,256]{2,1,0:T(8,128)S(1)}, f32[2,32,256]{2,1,0:T(8,128)S(1)}, u32[]{:S(2)}, u32[]{:S(2)}) collective-permute-start(f32[2,32,256]{2,1,0:T(8,128)S(1)} %pad_maximum_fusion.5), channel_id=1, source_target_pairs={{0,16},{16,0},{1,17},{17,1},{2,18},{18,2},{3,19},{19,3},{4,20},{20... | collective-permute-start | bytes 196616 | tf_op jit(solution)/shard_map/ppermute | solution.py:16
  316.4 49.9 %copy-start.6 = (bf16[3,1024,256]{2,1,0:T(8,128)(2,1)}, bf16[3,1024,256]{2,1,0:T(8,128)(2,1)S(1)}, u32[]{:S(2)}) copy-start(bf16[3,1024,256]{2,1,0:T(8,128)(2,1)S(1)} %broadcast_select_fusion.5) | copy-start | bytes 4718596
  316.5 49.6 %collective-permute-start.15 = (bf16[2,1024,256]{2,1,0:T(8,128)(2,1)S(1)}, bf16[2,1024,256]{2,1,0:T(8,128)(2,1)S(1)}, u32[]{:S(2)}, u32[]{:S(2)}) collective-permute-start(bf16[2,1024,256]{2,1,0:T(8,128)(2,1)S(1)} %slice.515), channel_id=1, source_target_pairs={{0,64},{64,0},{1,65},{65,1},{2,66},{66,2},{3,67},{67,3},{4,68},{68... | collective-permute-start | bytes 3145736 | tf_op jit(solution)/shard_map/ppermute | solution.py:16
  319.6 53.4 %copy-start.15 = (f32[2,32,256]{2,1,0:T(8,128)}, f32[2,32,256]{2,1,0:T(8,128)S(1)}, u32[]{:S(2)}) copy-start(f32[2,32,256]{2,1,0:T(8,128)S(1)} %collective-permute-done.10) | copy-start | bytes 196612
  319.8 19.4 %collective-permute-start.12 = (f32[2,32,256]{2,1,0:T(8,128)S(1)}, f32[2,32,256]{2,1,0:T(8,128)S(1)}, u32[]{:S(2)}, u32[]{:S(2)}) collective-permute-start(f32[2,32,256]{2,1,0:T(8,128)S(1)} %pad_maximum_fusion.6), channel_id=1, source_target_pairs={{0,32},{32,0},{1,33},{33,1},{2,34},{34,2},{3,35},{35,3},{4,36},{36... | collective-permute-start | bytes 196616 | tf_op jit(solution)/shard_map/ppermute | solution.py:16
  339.1 2.4 copy-start.16
  339.3 33.7 %collective-permute-start.14 = (f32[2,32,256]{2,1,0:T(8,128)S(1)}, f32[2,32,256]{2,1,0:T(8,128)S(1)}, u32[]{:S(2)}, u32[]{:S(2)}) collective-permute-start(f32[2,32,256]{2,1,0:T(8,128)S(1)} %pad_maximum_fusion.7), channel_id=1, source_target_pairs={{0,64},{64,0},{1,65},{65,1},{2,66},{66,2},{3,67},{67,3},{4,68},{68... | collective-permute-start | bytes 196616 | tf_op jit(solution)/shard_map/ppermute | solution.py:16
  366.3 29.9 %copy-start.9 = (bf16[2,1024,256]{2,1,0:T(8,128)(2,1)}, bf16[2,1024,256]{2,1,0:T(8,128)(2,1)S(1)}, u32[]{:S(2)}) copy-start(bf16[2,1024,256]{2,1,0:T(8,128)(2,1)S(1)} %broadcast_select_fusion.6) | copy-start | bytes 3145732
  366.4 29.8 %collective-permute-start.17 = (bf16[1,1024,256]{2,1,0:T(8,128)(2,1)S(1)}, bf16[1,1024,256]{2,1,0:T(8,128)(2,1)S(1)}, u32[]{:S(2)}, u32[]{:S(2)}) collective-permute-start(bf16[1,1024,256]{2,1,0:T(8,128)(2,1)S(1)} %slice.521), channel_id=1, source_target_pairs={{0,128},{128,0},{1,129},{129,1},{2,130},{130,2},{3,131},{131,3},{4... | collective-permute-start | bytes 1572872 | tf_op jit(solution)/shard_map/ppermute | solution.py:16
  372.9 24.1 %copy-start.17 = (f32[2,32,256]{2,1,0:T(8,128)}, f32[2,32,256]{2,1,0:T(8,128)S(1)}, u32[]{:S(2)}) copy-start(f32[2,32,256]{2,1,0:T(8,128)S(1)} %collective-permute-done.14) | copy-start | bytes 196612
  373.1 24.4 %collective-permute-start.16 = (f32[2,32,256]{2,1,0:T(8,128)S(1)}, f32[2,32,256]{2,1,0:T(8,128)}, u32[]{:S(2)}, u32[]{:S(2)}) collective-permute-start(f32[2,32,256]{2,1,0:T(8,128)S(1)} %pad_maximum_fusion.8), channel_id=1, source_target_pairs={{0,128},{128,0},{1,129},{129,1},{2,130},{130,2},{3,131},{131,3},{4... | collective-permute-start | bytes 196616 | tf_op jit(solution)/shard_map/ppermute | solution.py:16
  409.0 3.6 collective-permute-start.18
  412.6 7.3 %collective-permute-start.19 = (bf16[2,32,256]{2,1,0:T(8,128)(2,1)S(1)}, bf16[2,32,256]{2,1,0:T(8,128)(2,1)S(1)}, u32[]{:S(2)}, u32[]{:S(2)}) collective-permute-start(bf16[2,32,256]{2,1,0:T(8,128)(2,1)S(1)} %maximum_select_fusion.1), channel_id=1, source_target_pairs={{0,2},{2,0},{1,3},{3,1},{4,6},{6,4},{5,7},{7,5},{8,10},{10,8},{9,1... | collective-permute-start | bytes 98312 | tf_op jit(solution)/shard_map/ppermute | solution.py:16
where the time goes:
time: 430 us; the launch traced here: 427 us
  waiting for transfers between devices  328 us (76%)
  starting transfers between devices  34.9 us (8%)
  matrix products  22.2 us (5%)
  other arithmetic  20.5 us (5%)
  local copies, waits for them, and re-layouts  17.9 us (4%)
  between operations  4.34 us (1%)
    ppermute x20, waiting for transfers between devices, swapped(): return lax.ppermute(block, axis, route)  328 us
    ppermute x20, starting transfers between devices, swapped(): return lax.ppermute(block, axis, route)  34.9 us
    dot_general x8, matrix products, body(): jnp.dot(node_f, child_down, preferred_element_type=jnp.float32)  10.3 us
    unnamed x7, other arithmetic  9.51 us
    select_n x8, other arithmetic, spread_node_maps(): updated = jnp.where(taking[:, None, None], partner, moving)  9.18 us
  transfers between devices with their start and end apart: 20, of which 17 were waited for; matrix products, arithmetic and copies ran while one was open for 5% of the time, Pallas kernels for 0%

commit v1 on v0

v1 whole, which is shorter than its diff:
```python
import jax
import jax.numpy as jnp
import numpy as np
from jax import lax
from jax.experimental import pallas as pl
from jax.experimental.pallas import tpu as pltpu
from jax.sharding import PartitionSpec as P

MESH = pl.DeviceIdType.MESH
BF = jnp.bfloat16
F32 = jnp.float32
TILE = 256

SLOTS = (
    "W1", "R1", "B1", "W2", "V2", "R2", "B2", "B3", "W3", "R3", "W4", "R4", "B4", "B5",
    "W5", "R5", "W6", "R6", "B6", "R7", "B7", "W7", "V7", "S", "B8",
)
SLOT = {name: i for i, name in enumerate(SLOTS)}


def div(value, by):
    return lax.div(value, np.int32(by))


def rem(value, by):
    return lax.rem(value, np.int32(by))


def bit(value, i):
    return rem(div(value, 1 << i), 2)


def flip(value, mask):
    out = value
    for i in range(8):
        if mask >> i & 1:
            out = out + (1 - 2 * bit(value, i)) * (1 << i)
    return out


def mm(a, b):
    return jnp.dot(a, b, preferred_element_type=F32)


def kernel(
    rs_hbm, order_hbm, inv_hbm, vin_hbm, uout_hbm, lup_hbm, ldn_hbm,
    nup_hbm, ndn_hbm, ncr_hbm, lmap_hbm,
    out_ref,
    rs, order, inv, vin, lhs, sel, tree, uperm, nperm, fin,
    lmap, w0, r0, mats, comp, compx, route, ysend, yin, y2in,
    xsend, xin, x5in, zsend, zin, z7in, f5in, f3in, rex, cex,
    local_sem, send_sem, recv_sem,
):
    me = lax.axis_index("leaf")
    rank = w0.shape[0]
    points = rs.shape[1]
    rows = rs.shape[0]
    tiles = points // TILE

    is_y = rem(me, 8) == 1
    is_x = rem(me, 32) == 1
    level = [None] + [rem(me, 1 << k) == 1 << (k - 1) for k in range(1, 9)]
    ycen = div(me, 8) * 8 + 1
    xcen = div(me, 32) * 32 + 1
    ypos = rem(me, 8)
    xpos = rem(div(me, 8), 4)
    half = div(me, 128)
    neighbour = flip(me, 1)

    barrier = pltpu.get_barrier_semaphore()

    def greet(target):
        pl.semaphore_signal(barrier, inc=1, device_id=(target,), device_id_type=MESH)

    for r in range(1, 8):
        greet(flip(me, r))

    own4 = div(me, 16) * 16 + 8
    own5 = div(me, 32) * 32 + 16
    own6 = div(me, 64) * 64 + 32

    @pl.when(is_y)
    def _():
        for r in range(1, 4):
            greet(flip(me, 8 * r))
        greet(own4)
        greet(own5)

    @pl.when(is_x)
    def _():
        for r in range(1, 8):
            greet(flip(me, 32 * r))
        greet(own6)
        greet(64)
        greet(192)
        greet(128)

    def fetch(src, dst, i):
        return pltpu.make_async_copy(src, dst, local_sem.at[i])

    loads = [
        fetch(order_hbm, order, 0),
        fetch(rs_hbm, rs, 1),
        fetch(vin_hbm, vin, 2),
        fetch(lmap_hbm, lmap, 3),
        fetch(lup_hbm, w0, 4),
        fetch(inv_hbm, inv, 5),
        fetch(uout_hbm, lhs.at[pl.ds(0, rank)], 6),
        fetch(ldn_hbm, r0, 7),
    ]
    for load in loads:
        load.start()

    counter = [0]
    sent = {}

    def slot_of(name):
        return mats.at[SLOT[name]]

    n_mats = len(SLOTS)
    recv_at = {}
    base = n_mats
    for name, count in (
        ("route", 4), ("yin", 8), ("y2in", 8), ("xin", 4), ("x5in", 4),
        ("zin", 8), ("z7in", 8), ("f5in", 1), ("f3in", 1), ("rex", 4), ("cex", 4),
    ):
        recv_at[name] = base
        base += count

    def send(role, src, dst, rsem, target):
        i = counter[0]
        counter[0] += 1
        pltpu.make_async_remote_copy(
            src_ref=src, dst_ref=dst, send_sem=send_sem.at[i], recv_sem=recv_sem.at[rsem],
            device_id=(target,), device_id_type=MESH,
        ).start()
        sent.setdefault(role, []).append((i, dst.shape[0] == rank))

    def arrived(dst, rsem):
        pltpu.make_async_remote_copy(
            src_ref=dst, dst_ref=dst, send_sem=send_sem.at[0], recv_sem=recv_sem.at[rsem],
            device_id=(neighbour,), device_id_type=MESH,
        ).wait_recv()

    def need(*names):
        for name in names:
            arrived(slot_of(name), SLOT[name])

    def ship(role, name, src, target):
        send(role, src, slot_of(name), SLOT[name], target)

    def keep(name, src):
        pltpu.make_async_copy(src, slot_of(name), recv_sem.at[SLOT[name]]).start()

    left = ncr_hbm.at[pl.ds(0, rank)]
    right = ncr_hbm.at[pl.ds(rank, rank)]

    loads[0].wait()
    loads[1].wait()

    def gather(t, carry):
        cols = pl.ds(pl.multiple_of(t * TILE, TILE), TILE)
        ids = lax.broadcasted_iota(jnp.int32, (points, TILE), 0)
        hot = jnp.where(ids == order[:, cols], 1.0, 0.0).astype(BF)
        sel[:, cols] = hot
        tree[:, cols] = mm(rs[...], hot).astype(BF)
        return carry

    lax.fori_loop(0, tiles, gather, 0)

    n_in = (
        7
        + jnp.where(is_y, 3, 0)
        + jnp.where(is_x, 7, 0)
        + jnp.where(level[4], 2, 0)
        + jnp.where(level[5], 4, 0)
        + jnp.where(level[6], 2, 0)
        + jnp.where(level[7], 8, 0)
        + jnp.where(level[8], 8, 0)
    )
    pl.semaphore_wait(barrier, n_in)

    left2 = rem(me, 8) == 2
    right2 = rem(me, 8) == 6

    @pl.when(left2)
    def _():
        ship("L2l", "W2", nup_hbm, me - 1)

    @pl.when(right2)
    def _():
        ship("L2r", "V2", nup_hbm, me - 5)

    @pl.when(level[1])
    def _():
        ship("L1", "W1", nup_hbm, me - 1)
        keep("W1", nup_hbm)

    @pl.when(level[3])
    def _():
        ship("L3", "W3", nup_hbm, me - 3)

    @pl.when(level[4])
    def _():
        for target, side in ((me - 7, left), (me + 1, right)):
            ship("L4", "W4", nup_hbm, target)
            ship("L4", "R4", ndn_hbm, target)
            ship("L4", "B4", side, target)

    @pl.when(level[5])
    def _():
        ship("L5", "W5", nup_hbm, me - 15)
        ship("L5", "R5", ndn_hbm, me - 15)
        for i in range(4):
            ship("L5", "B5", left if i < 2 else right, me - 15 + 8 * i)

    @pl.when(level[6])
    def _():
        for i in range(2):
            ship("L6", "W6", nup_hbm, me - 31 + 32 * i)
        for i in range(2):
            ship("L6", "R6", ndn_hbm, me - 31 + 32 * i)
            ship("L6", "B6", left if i < 1 else right, me - 31 + 32 * i)

    @pl.when(level[7])
    def _():
        for i in range(4):
            ship("L7", "V7", nup_hbm, (1 - half) * 128 + 1 + 32 * i)
        for i in range(4):
            target = half * 128 + 1 + 32 * i
            ship("L7", "R7", ndn_hbm, target)
            ship("L7", "W7", nup_hbm, target)
            ship("L7", "B7", left if i < 2 else right, target)

    @pl.when(level[8])
    def _():
        for i in (0, 7, 1, 6, 2, 5, 3, 4):
            target = 1 + 32 * i
            ship("L8", "S", nup_hbm, target)
            ship("L8", "B8", left if i < 4 else right, target)

    loads[2].wait()
    route[0] = mm(tree[...], vin[...]).astype(BF)
    for r in (3, 2, 1):
        send("all", route.at[0], route.at[r], recv_at["route"] + r, flip(me, r))

    @pl.when(level[1])
    def _():
        ship("L1", "R1", ndn_hbm, me - 1)
        keep("R1", ndn_hbm)
        ship("L1", "B1", left, me - 1)
        keep("B1", right)

    loads[4].wait()
    need("W1")
    comp[0] = mm(w0[...], slot_of("W1")[...]).astype(BF)

    loads[3].wait()
    source = np.int32(0)
    for r in range(1, 4):
        source = jnp.where(lmap[flip(me, r)] == me, r, source)
    for r in range(1, 4):
        arrived(route.at[r], recv_at["route"] + r)
    g0 = route[source]
    ysend[0] = g0
    ysend[2] = mm(g0, comp[0]).astype(BF)

    @pl.when(jnp.logical_not(is_y))
    def _():
        send("notY", ysend.at[2], y2in.at[ypos], recv_at["y2in"] + ypos, ycen)

    ysend[1] = mm(g0, w0[...]).astype(BF)
    for r in (7, 6, 5, 4, 3, 2, 1):
        k = 2 if r >= 4 else 1 if r >= 2 else 0
        send("all", ysend.at[k], yin.at[r], recv_at["yin"] + r, flip(me, r))

    @pl.when(level[2])
    def _():
        keep("R2", ndn_hbm)
        keep("B2", right)
        for r in (3, 2, 1):
            ship("L2", "R2", ndn_hbm, flip(me, r))
            ship("L2", "B2", right if r == 1 else left, flip(me, r))

    @pl.when(level[3])
    def _():
        ship("L3", "R3", ndn_hbm, me - 3)
        for i in range(8):
            src = left if i < 4 else right
            if i == 4:
                keep("B3", src)
            else:
                ship("L3", "B3", src, me + (i - 4))

    loads[5].wait()

    def near(t, carry):
        cols = pl.ds(pl.multiple_of(t * TILE, TILE), TILE)
        value = mm(tree[...], inv[:, cols])
        high = value.astype(BF)
        lhs[pl.ds(rank, rows), cols] = high
        lhs[pl.ds(rank + rows, rows), cols] = (value - high.astype(F32)).astype(BF)
        return carry

    lax.fori_loop(0, tiles, near, 0)

    @pl.when(is_y)
    def _():
        need("W3", "W4")
        compx[0] = mm(slot_of("W3")[...], slot_of("W4")[...]).astype(BF)
        need("W2", "V2")
        total = ysend[2].astype(F32)
        for i in (0, 2, 3):
            arrived(y2in.at[i], recv_at["y2in"] + i)
            total = total + y2in[i].astype(F32)
        g3 = mm(total.astype(BF), slot_of("W2")[...])
        for i in (4, 5, 6, 7):
            arrived(y2in.at[i], recv_at["y2in"] + i)
        total = (
            y2in[4].astype(F32) + y2in[5].astype(F32) + y2in[6].astype(F32) + y2in[7].astype(F32)
        )
        g3 = (g3 + mm(total.astype(BF), slot_of("V2")[...])).astype(BF)
        xsend[0] = g3
        xsend[2] = mm(g3, compx[0]).astype(BF)

        @pl.when(jnp.logical_not(is_x))
        def _():
            send("YnotX", xsend.at[2], x5in.at[xpos], recv_at["x5in"] + xpos, xcen)

        xsend[1] = mm(g3, slot_of("W3")[...]).astype(BF)
        for r in (3, 2, 1):
            send("Y", xsend.at[1 if r >= 2 else 0], xin.at[r], recv_at["xin"] + r, flip(me, 8 * r))

    loads[6].wait()

    def scatter(t, carry):
        cols = pl.ds(pl.multiple_of(t * TILE, TILE), TILE)
        both = lax.dot_general(
            lhs[...], sel[cols, :], (((1,), (1,)), ((), ())), preferred_element_type=F32
        )
        uperm[:, cols] = both[:rank].astype(BF)
        nperm[:, cols] = both[rank : rank + rows] + both[rank + rows :]
        return carry

    lax.fori_loop(0, tiles, scatter, 0)

    @pl.when(is_x)
    def _():
        need("W5", "W6")
        compx[1] = mm(slot_of("W5")[...], slot_of("W6")[...]).astype(BF)
        total = xsend[2].astype(F32)
        for s in range(1, 4):
            arrived(x5in.at[s], recv_at["x5in"] + s)
            total = total + x5in[s].astype(F32)
        g5 = total.astype(BF)
        zsend[0] = g5
        zsend[2] = mm(g5, compx[1]).astype(BF)
        for r in (4, 5, 6, 7, 3, 2, 1):
            send("X", zsend.at[2], z7in.at[r], recv_at["z7in"] + r, flip(me, 32 * r))
        zsend[1] = mm(g5, slot_of("W5")[...]).astype(BF)
        for r in (3, 2, 1):
            send("X", zsend.at[1 if r >= 2 else 0], zin.at[r], recv_at["zin"] + r, flip(me, 32 * r))

    loads[7].wait()
    need("R1")
    comp[0] = mm(slot_of("R1")[...], r0[...]).astype(BF)
    need("R2")
    rex[0] = mm(slot_of("R2")[...], comp[0]).astype(BF)
    for r in (3, 2, 1):
        send("all", rex.at[0], rex.at[r], recv_at["rex"] + r, flip(me, r))
    for r in range(1, 8):
        arrived(yin.at[r], recv_at["yin"] + r)
    need("B3", "B2", "B1")
    g2 = yin[4].astype(F32) + yin[5].astype(F32) + yin[6].astype(F32) + yin[7].astype(F32)
    g1 = yin[2].astype(F32) + yin[3].astype(F32)
    part = mm(g2.astype(BF), slot_of("B3")[...]).astype(BF)
    part = (mm(g1.astype(BF), slot_of("B2")[...]) + mm(part, slot_of("R1")[...])).astype(BF)
    cex[0] = (mm(yin[1], slot_of("B1")[...]) + mm(part, r0[...])).astype(BF)
    for r in (3, 2, 1):
        send("all", cex.at[0], cex.at[r], recv_at["cex"] + r, flip(me, r))

    @pl.when(is_y)
    def _():
        need("R3", "R4", "B4", "B5")
        compx[2] = mm(slot_of("R4")[...], slot_of("R3")[...]).astype(BF)
        for r in range(1, 4):
            arrived(xin.at[r], recv_at["xin"] + r)
        g4 = (xin[2].astype(F32) + xin[3].astype(F32)).astype(BF)
        upper = mm(g4, slot_of("B5")[...]).astype(BF)
        fin[:, pl.ds(0, rank)] = mm(xin[1], slot_of("B4")[...]) + mm(upper, slot_of("R3")[...])

    @pl.when(is_x)
    def _():
        need("R5", "R6", "B6", "B7", "R7", "S", "W7", "V7", "B8")
        r65 = mm(slot_of("R6")[...], slot_of("R5")[...]).astype(BF)
        compx[3] = mm(slot_of("B7")[...], slot_of("R5")[...]).astype(BF)
        top = mm(slot_of("S")[...], slot_of("R7")[...]).astype(BF)
        top = mm(top, r65).astype(BF)
        compx[4] = mm(slot_of("W7")[...], top).astype(BF)
        compx[5] = (mm(slot_of("V7")[...], top) + mm(slot_of("B8")[...], r65)).astype(BF)
        for r in range(1, 4):
            arrived(zin.at[r], recv_at["zin"] + r)
        g6 = (zin[2].astype(F32) + zin[3].astype(F32)).astype(BF)
        value = mm(zin[1], slot_of("B6")[...]) + mm(g6, compx[3])
        g7 = zsend[2].astype(F32)
        for r in range(1, 4):
            arrived(z7in.at[r], recv_at["z7in"] + r)
            g7 = g7 + z7in[r].astype(F32)
        value = value + mm(g7.astype(BF), compx[4])
        for r in range(4, 8):
            arrived(z7in.at[r], recv_at["z7in"] + r)
        g7 = (
            z7in[4].astype(F32) + z7in[5].astype(F32) + z7in[6].astype(F32) + z7in[7].astype(F32)
        )
        value = value + mm(g7.astype(BF), compx[5])
        f5in[...] = value.astype(BF)
        for r in (2, 3, 1):
            send("X", f5in, f5in, recv_at["f5in"], flip(me, 8 * r))

    @pl.when(is_y)
    def _():
        @pl.when(jnp.logical_not(is_x))
        def _():
            arrived(f5in, recv_at["f5in"])

        f3in[...] = (mm(f5in[...], compx[2]) + fin[:, pl.ds(0, rank)]).astype(BF)
        for r in (5, 4, 7, 6, 3, 2, 1):
            send("Y", f3in, f3in, recv_at["f3in"], flip(me, r))

    for r in range(1, 4):
        arrived(rex.at[r], recv_at["rex"] + r)
    for r in range(1, 4):
        arrived(cex.at[r], recv_at["cex"] + r)
    place = lmap[me]
    pick = np.int32(0)
    for r in range(1, 4):
        pick = jnp.where(place == flip(me, r), r, pick)
    down = rex[pick]
    cross = cex[pick]

    def close(t, carry):
        cols = pl.ds(pl.multiple_of(t * TILE, TILE), TILE)
        nperm[:, cols] = nperm[:, cols] + mm(cross, uperm[:, cols])
        uperm[:, cols] = mm(down, uperm[:, cols]).astype(BF)
        return carry

    lax.fori_loop(0, tiles, close, 0)

    @pl.when(jnp.logical_not(is_y))
    def _():
        arrived(f3in, recv_at["f3in"])

    out_ref[...] = nperm[...] + mm(f3in[...], uperm[...])

    def drain(role):
        for i, is_square in sent.get(role, []):
            like = mats.at[0] if is_square else route.at[0]
            pltpu.make_async_remote_copy(
                src_ref=like, dst_ref=like, send_sem=send_sem.at[i], recv_sem=recv_sem.at[0],
                device_id=(neighbour,), device_id_type=MESH,
            ).wait_send()

    drain("all")
    for role, cond in (
        ("notY", jnp.logical_not(is_y)),
        ("YnotX", jnp.logical_and(is_y, jnp.logical_not(is_x))),
        ("Y", is_y), ("X", is_x),
        ("L1", level[1]), ("L2l", left2), ("L2r", right2), ("L2", level[2]), ("L3", level[3]), ("L4", level[4]),
        ("L5", level[5]), ("L6", level[6]), ("L7", level[7]), ("L8", level[8]),
    ):
        @pl.when(cond)
        def _(role=role):
            drain(role)

    assert counter[0] <= send_sem.shape[0], counter[0]
    assert base <= recv_sem.shape[0], base


def solution(mesh):
    def body(
        right_sides, point_order, leaf_inverse, basis_in, basis_out, leaf_up, leaf_down,
        node_up, node_down, node_cross, leaf_map,
    ):
        rows, points = right_sides.shape
        rank = leaf_up.shape[0]
        small = (rows, rank)
        square = (rank, rank)
        anywhere = pl.BlockSpec(memory_space=pl.ANY)
        return pl.pallas_call(
            kernel,
            out_shape=pltpu.VMEM((rows, points), F32),
            in_specs=[anywhere] * 11,
            out_specs=pl.BlockSpec(memory_space=pltpu.VMEM),
            scratch_shapes=[
                pltpu.VMEM((rows, points), BF),
                pltpu.VMEM((1, points), jnp.int32),
                pltpu.VMEM((points, points), BF),
                pltpu.VMEM((points, rank), BF),
                pltpu.VMEM((rank + 2 * rows, points), BF),
                pltpu.VMEM((points, points), BF),
                pltpu.VMEM((rows, points), BF),
                pltpu.VMEM((rank, points), BF),
                pltpu.VMEM((rows, points), F32),
                pltpu.VMEM(small, F32),
                pltpu.SMEM(leaf_map.shape, jnp.int32),
                pltpu.VMEM(square, BF),
                pltpu.VMEM(square, BF),
                pltpu.VMEM((len(SLOTS),) + square, BF),
                pltpu.VMEM((2,) + square, BF),
                pltpu.VMEM((6,) + square, BF),
                pltpu.VMEM((4,) + small, BF),
                pltpu.VMEM((4,) + small, BF),
                pltpu.VMEM((8,) + small, BF),
                pltpu.VMEM((8,) + small, BF),
                pltpu.VMEM((3,) + small, BF),
                pltpu.VMEM((4,) + small, BF),
                pltpu.VMEM((4,) + small, BF),
                pltpu.VMEM((3,) + small, BF),
                pltpu.VMEM((8,) + small, BF),
                pltpu.VMEM((8,) + small, BF),
                pltpu.VMEM(small, BF),
                pltpu.VMEM(small, BF),
                pltpu.VMEM((4,) + square, BF),
                pltpu.VMEM((4,) + small, BF),
                pltpu.SemaphoreType.DMA((8,)),
                pltpu.SemaphoreType.DMA((128,)),
                pltpu.SemaphoreType.DMA((80,)),
            ],
            compiler_params=pltpu.CompilerParams(
                collective_id=0, has_side_effects=True, vmem_limit_bytes=56 * 1024 * 1024
            ),
        )(
            right_sides, point_order, leaf_inverse, basis_in, basis_out, leaf_up, leaf_down,
            node_up, node_down, node_cross, leaf_map,
        )

    placed = (P(None, "leaf"),) + (P("leaf", None),) * 9 + (P(),)
    return jax.shard_map(
        body, mesh=mesh, in_specs=placed, out_specs=P(None, "leaf"), check_vma=False
    )
```

time: 430 us -> 33.7 us (0.08)
  waiting for transfers between devices: 328 us -> 0 us
  starting transfers between devices: 34.9 us -> 0 us
  Pallas kernels: 0 us -> 32.9 us
  matrix products: 22.2 us -> 0 us
  other arithmetic: 20.5 us -> 0 us
  local copies, waits for them, and re-layouts: 17.9 us -> 0.71 us
  between operations: 4.34 us -> 0.01 us
    ppermute x20 -> x0, waiting for transfers between devices: 328 us -> none  [swapped(): return lax.ppermute(block, axis, route)]
    ppermute x20 -> x0, starting transfers between devices: 34.9 us -> none  [swapped(): return lax.ppermute(block, axis, route)]
    pallas_call x0 -> x1, Pallas kernels: none -> 32.9 us  [body(): pl.pallas_call(kernel, out_shape=pltpu.VMEM((rows, points), F32), in_spec...]
    dot_general x20 -> x0, matrix products: 22.2 us -> none  [the longest x8 10.3 us: body(): jnp.dot(node_f, child_down, preferred_element_type=jnp.float32)]
    unnamed x7 -> x0, other arithmetic: 9.51 us -> none
    select_n x11 -> x0, other arithmetic: 9.21 us -> none  [the longest x8 9.18 us: spread_node_maps(): updated = jnp.where(taking[:, None, None], partner, moving)]
    scatter x2 -> x0, local copies, waits for them, and re-layouts: 6.86 us -> none  [body(): return jnp.zeros_like(answer).at[:, ordering].set(answer)]
    gather x1 -> x0, local copies, waits for them, and re-layouts: 6.18 us -> none  [body(): tree_rhs = jnp.take(right_sides, ordering, axis=1)]
  transfers between devices with their start and end apart: 20 -> 0, of which waited for: 17 -> 0; matrix products, arithmetic and copies ran while one was open for 5% -> 0% of each run, Pallas kernels for 0% -> 0%
where the time goes in v1:
time: 33.7 us; the launch traced here: 33.6 us
  Pallas kernels  32.9 us (98%)
  local copies, waits for them, and re-layouts  0.71 us (2%)
    pallas_call x1, Pallas kernels, body(): pl.pallas_call(kernel, out_shape=pltpu.VMEM((rows, points), F32), in_spec...  32.9 us
    unnamed x1, local copies, waits for them, and re-layouts  0.71 us

profile of v1, /device:TPU:11, one launch (start us, length us, event | category | flops | bytes accessed | tf_op | source)
XLA Modules:
  0.0 33.6 jit_solution(7971025737263981119)
XLA Ops:
  0.0 32.9 %shard_map.109 = f32[32,2048]{1,0:T(8,128)S(1)} custom-call(bf16[32,2048]{1,0:T(8,128)(2,1)} %rs_hbm.1, s32[1,2048]{1,0:T(1,128)} %order_hbm.1, bf16[2048,2048]{1,0:T(8,128)(2,1)} %inv_hbm.1, bf16[2048,256]{1,0:T(8,128)(2,1)} %vin_hbm.1, bf16[256,2048]{1,0:T(8,128)(2,1)} %uout_hbm.1, bf16[256,256]{1,0:T(8,128)(2,1)} %lup_hbm.1, bf16[256,256]{1,0:T(8,128)(2,1)} %ldn_hbm.1, ...), custom_call_target="tpu_custom_call" | custom-call | tf_op jit(solution)/shard_map/pallas_call | solution.py:489
  32.9 0.7 %copy.13 = f32[32,2048]{1,0:T(8,128)} copy(f32[32,2048]{1,0:T(8,128)S(1)} %shard_map.109) | data formatting | bytes 524288
